TPU v7x, 32 devices: a whole 2x2x4 slice. The times are simulated.
32 devices in a mesh: group: 2 (over y), view: 4 (over z), depth: 2 (over x), row: 2 (over core).
Axes of the slice: x: 2, y: 2, z: 4, core: 2. Of those that a mesh axis runs over, the one named last changes fastest.
Arguments:
- features: float32 [4, 32, 8, 512], P('view', None, ('group', 'row')), parts along dimension 2, may hold values from -6 to 6
- cotangent: float32 [8, 32, 8, 512], P('depth', 'view', ('group', 'row')), parts along dimension 2, may hold values from -6 to 6
- src_row: int32 [4, 8, 8, 512], P('view', 'depth', ('group', 'row')), parts along dimension 2, may hold values from -2 to 4, as said below
- src_col: int32 [4, 8, 8, 512], P('view', 'depth', ('group', 'row')), parts along dimension 2, may hold values from 0 to 510
- fractions: int32 [2, 4, 8, 8, 512], P(None, 'view', 'depth', ('group', 'row')), parts along dimension 3, may hold values from 0 to 256
Outputs:
- grad_features: float32 [4, 32, 8, 512], P('view', None, ('group', 'row'), 'depth'), parts along dimension 2
There are 2 independent parts, one for each index of `group`. A program takes and returns all parts, laid end to end along the dimension named above; each array names one. Nothing has to cross between parts.
Inputs may be any that keep to these rules, and one draw needn't show every extreme that they name: src_row[v, d, y, x] lies between y - 2 and y + 1.
All inputs are finite; a program needn't handle non-finite values.
Results may differ from a plain program's by a relative error of at most 0.0003.
Values sent between devices are 32-bit elements; how exact they have to be, the bound alone decides.
A program may use at most 64 MiB of HBM per device.

v0:
```python
import jax
import jax.numpy as jnp
from jax import lax
from jax.sharding import PartitionSpec as P

HALO = 2


def partner(shard, axis, apart):
    return lax.ppermute(shard, axis, [(i, i ^ 1 << apart) for i in range(lax.axis_size(axis))])


def with_halo(block, sides, width):
    for axis, dim in sides:
        count = lax.axis_size(axis)
        forward = [(i, i + 1) for i in range(count - 1)]
        backward = [(target, source) for source, target in forward]
        low = lax.ppermute(
            lax.slice_in_dim(block, block.shape[dim] - width, None, axis=dim), axis, forward
        )
        high = lax.ppermute(lax.slice_in_dim(block, 0, width, axis=dim), axis, backward)
        block = jnp.concatenate([low, block, high], axis=dim)
    return block


def sample(flattened, flat_index, frac_row, frac_col, width):

    def corner(shift_by):
        return jnp.take(flattened, flat_index + shift_by, axis=1)

    upper_mix = (1.0 - frac_col) * corner(0) + frac_col * corner(1)
    lower_mix = (1.0 - frac_col) * corner(width) + frac_col * corner(width + 1)
    mixed = (1.0 - frac_row) * upper_mix + frac_row * lower_mix
    return jnp.transpose(mixed, (1, 0, 2, 3))


def spread(grad_warp, flat_index, frac_row, frac_col, width, length):
    moved = jnp.transpose(grad_warp, (1, 0, 2, 3))
    channels = moved.shape[0]
    upper_part = (1.0 - frac_row) * moved
    lower_part = frac_row * moved
    result = jnp.zeros((channels, length), jnp.float32)
    result = result.at[:, flat_index].add((1.0 - frac_col) * upper_part)
    result = result.at[:, flat_index + 1].add(frac_col * upper_part)
    result = result.at[:, flat_index + width].add((1.0 - frac_col) * lower_part)
    result = result.at[:, flat_index + width + 1].add(frac_col * lower_part)
    return result


def fold_rims(grad_pad):
    upper_rim = grad_pad[:, :HALO]
    lower_rim = grad_pad[:, grad_pad.shape[1] - HALO :]
    interior = grad_pad[:, HALO : grad_pad.shape[1] - HALO]
    is_first = lax.axis_index("row") == 0
    outgoing = jnp.where(is_first, lower_rim, upper_rim)
    incoming = partner(outgoing, "row", 0)
    add_upper = jnp.where(is_first, 0.0, incoming)
    add_lower = jnp.where(is_first, incoming, 0.0)
    interior = interior.at[:, :HALO].add(add_upper)
    interior = interior.at[:, interior.shape[1] - HALO :].add(add_lower)
    return interior


def depth_reduce(partial_grad):
    return lax.psum_scatter(partial_grad, "depth", scatter_dimension=2, tiled=True)


def per_device(features, cotangent, src_row, src_col, fractions):
    channels = features.shape[1]
    row_count = features.shape[2]
    col_count = features.shape[3]
    padded = with_halo(features[0], (("row", 1),), HALO)
    padded_rows = row_count + 2 * HALO
    flattened = padded.reshape(channels, padded_rows * col_count)
    row_offset = lax.axis_index("row") * row_count
    flat_index = (src_row[0] - row_offset + HALO) * col_count + src_col[0]
    weights = fractions[:, 0].astype(jnp.float32) / 256.0
    warped = sample(flattened, flat_index, weights[0], weights[1], col_count)
    view_count = lax.axis_size("view") * features.shape[0]
    factor = 2.0 / view_count
    full_cotangent = lax.all_gather(cotangent, "view", axis=1, tiled=True)
    view_sum = lax.psum(warped, "view")
    average = view_sum / view_count
    grad_warp = factor * full_cotangent * (warped - average)
    spread_out = spread(
        grad_warp, flat_index, weights[0], weights[1], col_count, padded_rows * col_count
    )
    grad_pad = spread_out.reshape(channels, padded_rows, col_count)
    result = fold_rims(depth_reduce(grad_pad))
    return result[None]


def solution(mesh):
    in_specs = (
        P("view", None, ("group", "row"), None),
        P("depth", "view", ("group", "row"), None),
        P("view", "depth", ("group", "row"), None),
        P("view", "depth", ("group", "row"), None),
        P(None, "view", "depth", ("group", "row"), None),
    )
    out_specs = P("view", None, ("group", "row"), "depth")
    return jax.shard_map(
        per_device, mesh=mesh, in_specs=in_specs, out_specs=out_specs, check_vma=False
    )
```

profile of v0, /device:TPU:0, one launch (start us, length us, event | category | flops | bytes accessed | tf_op | source)
XLA Modules:
  0.0 254.8 jit_solution(4598418391159267502)
XLA Ops:
  6.5 0.0 all-reduce.2.cloned.1.call-start
  6.5 2.4 collective-permute-start
  8.9 1.3 collective-permute-start.1
  10.2 0.8 fusion.13
  11.1 0.1 compare_and_fusion.3
  11.2 0.8 convert_multiply_fusion
  12.1 0.0 collective-permute-done
  12.1 0.3 collective-permute-done.1
  12.4 1.1 pad_maximum_fusion
  13.5 0.5 copy.12
  14.0 14.1 %gather_fusion = f32[4096,32]{1,0:T(8,128)} fusion(f32[32,3072]{0,1:T(8,128)S(1)} %bitcast.135, s32[4096]{0:T(1024)S(1)} %broadcast_clamp_fusion.3), kind=kCustom, calls=%fused_computation.clone | custom fusion | bytes 1064960 | tf_op jit(solution)/shard_map/jit(_take)/gather | solution.py:29
  28.1 1.9 copy.13
  30.0 14.1 %gather_fusion.1 = f32[4096,32]{1,0:T(8,128)} fusion(f32[32,3072]{0,1:T(8,128)S(1)} %bitcast.136, s32[4096]{0:T(1024)S(1)} %broadcast_clamp_fusion.2), kind=kCustom, calls=%fused_computation.1.clone | custom fusion | bytes 1064960 | tf_op jit(solution)/shard_map/jit(_take)/gather | solution.py:29
  44.1 1.9 copy.14
  46.0 14.1 %gather_fusion.2 = f32[4096,32]{1,0:T(8,128)} fusion(f32[32,3072]{0,1:T(8,128)S(1)} %bitcast.137, s32[4096]{0:T(1024)S(1)} %broadcast_clamp_fusion.1), kind=kCustom, calls=%fused_computation.2.clone | custom fusion | bytes 1064960 | tf_op jit(solution)/shard_map/jit(_take)/gather | solution.py:29
  60.1 1.9 copy.15
  62.0 14.1 %gather_fusion.3 = f32[4096,32]{1,0:T(8,128)} fusion(f32[32,3072]{0,1:T(8,128)S(1)} %bitcast.138, s32[4096]{0:T(1024)S(1)} %broadcast_clamp_fusion), kind=kCustom, calls=%fused_computation.3.clone | custom fusion | bytes 1064960 | tf_op jit(solution)/shard_map/jit(_take)/gather | solution.py:29
  76.0 1.9 copy.16
  77.9 0.0 copy-start
  78.0 1.7 fusion.5
  79.7 0.0 all-reduce.2.cloned.1.call-update
  79.7 0.0 reduce-scatter.2.cloned.1.call-start
  79.9 0.0 copy-done
  79.9 22.9 %all_gather.3 = f32[4,32,2,512]{3,2,1,0:T(2,128)S(1)} all-gather(f32[4,8,2,512]{3,2,1,0:T(2,128)S(1)} %copy-done), channel_id=1, replica_groups=mesh['group'=2,'view'=4,'depth'=2,'row'=2] {'view'}, dimensions={1}, use_global_device_ids=true | all-gather | bytes 655360 | tf_op jit(solution)/shard_map/all_gather | solution.py:81
  102.7 22.7 %all-reduce.2.cloned.1.call-done = f32[4,32,2,512]{3,2,1,0:T(2,128)} async-done(((f32[4,32,2,512]{3,2,1,0:T(2,128)}), f32[4,32,2,512]{3,2,1,0:T(2,128)}) %all-reduce.2.cloned.1.call-update) | async-done | bytes 524304 | tf_op jit(solution)/shard_map/psum | solution.py:82
  125.4 1.8 multiply_bitcast_fusion
  127.2 0.6 multiply_bitcast_fusion.1
  127.9 1.8 copy.26
  129.6 1.7 copy.27
  131.4 1.8 copy.28
  133.1 1.7 copy.29
  134.9 23.0 %scatter_custom_fusion = f32[32,3072]{0,1:T(8,128)S(1)} fusion(s32[4096]{0:T(1024)S(1)} %bitcast.158, f32[4096,32]{1,0:T(8,128)} %bitcast.147, f32[]{:T(128)} %constant.99.clone.1), kind=kCustom, calls=%fused_computation.8 | custom fusion | flops 131072 | bytes 393728 | tf_op jit(solution)/shard_map/scatter-add | solution.py:43
  157.9 23.3 %scatter_fusion = f32[32,3072]{0,1:T(8,128)S(1)} fusion(f32[32,3072]{0,1:T(8,128)S(1)} %scatter_custom_fusion, s32[4096]{0:T(1024)S(1)} %bitcast.153, f32[4096,32]{1,0:T(8,128)} %bitcast.142), kind=kCustom, calls=%fused_computation.5 | custom fusion | flops 131072 | bytes 1589248 | tf_op jit(solution)/shard_map/scatter-add | solution.py:44
  181.2 23.3 %scatter_fusion.1 = f32[32,3072]{0,1:T(8,128)S(1)} fusion(f32[32,3072]{0,1:T(8,128)S(1)} %scatter_fusion, s32[4096]{0:T(1024)S(1)} %bitcast.152, f32[4096,32]{1,0:T(8,128)} %bitcast.141), kind=kCustom, calls=%fused_computation.6 | custom fusion | flops 131072 | bytes 1589248 | tf_op jit(solution)/shard_map/scatter-add | solution.py:45
  204.4 23.4 %scatter_fusion.2 = f32[32,3072]{0,1:T(8,128)S(1)} fusion(f32[32,3072]{0,1:T(8,128)S(1)} %scatter_fusion.1, s32[4096]{0:T(1024)S(1)} %bitcast.151, f32[4096,32]{1,0:T(8,128)} %bitcast.140), kind=kCustom, calls=%fused_computation.7 | custom fusion | flops 131072 | bytes 1589248 | tf_op jit(solution)/shard_map/scatter-add | solution.py:46
  227.9 1.5 copy.25
  229.3 0.0 reduce-scatter.2.cloned.1.call-update
  229.4 14.6 %reduce-scatter.2.cloned.1.call-done = f32[32,6,256]{2,1,0:T(8,128)} async-done(((f32[32,6,512]{2,1,0:T(8,128)}), f32[32,6,256]{2,1,0:T(8,128)}) %reduce-scatter.2.cloned.1.call-update) | async-done | bytes 196624 | tf_op jit(solution)/shard_map/reduce_scatter | solution.py:65
  243.9 1.1 slice_select_fusion
  245.0 0.1 collective-permute-start.2
  245.1 1.2 collective-permute-done.2
  246.4 1.6 fusion.9
  (15 shorter events, 0.2 us)
Async XLA Ops:
  6.5 118.9 %all-reduce.2.cloned.1.call-start = ((), (), s32[]{:S(2)}) async-start(), calls=%async_computation.1 | async-start | bytes 1048576 | tf_op jit(solution)/shard_map/psum | solution.py:82
  6.5 5.5 %collective-permute-start = (f32[32,2,512]{2,1,0:T(2,128)}, f32[32,2,512]{2,1,0:T(2,128)S(1)}, u32[]{:S(2)}, u32[]{:S(2)}) collective-permute-start(f32[32,2,512]{2,1,0:T(2,128)} %bitcast.148), channel_id=1, source_target_pairs={{0,1},{2,3},{4,5},{6,7},{8,9},{10,11},{12,13},{14,15},{16,17},{18,... | collective-permute-start | bytes 393224 | tf_op jit(solution)/shard_map/ppermute | solution.py:18
  8.9 3.5 %collective-permute-start.1 = (f32[32,2,512]{2,1,0:T(2,128)}, f32[32,2,512]{2,1,0:T(2,128)S(1)}, u32[]{:S(2)}, u32[]{:S(2)}) collective-permute-start(f32[32,2,512]{2,1,0:T(2,128)} %bitcast.149), channel_id=1, source_target_pairs={{1,0},{3,2},{5,4},{7,6},{9,8},{11,10},{13,12},{15,14},{17,16},{19,... | collective-permute-start | bytes 393224 | tf_op jit(solution)/shard_map/ppermute | solution.py:21
  77.9 1.9 copy-start
  79.7 164.2 %reduce-scatter.2.cloned.1.call-start = ((), (), s32[]{:S(2)}) async-start(), calls=%async_computation.2 | async-start | bytes 786432 | tf_op jit(solution)/shard_map/reduce_scatter | solution.py:65
  245.0 1.3 collective-permute-start.2
Sparse Core Ops, SparseCore 0:
  79.8 45.5 all-reduce.1
  229.5 14.4 reduce-scatter.1
where the time goes:
time: 255 us
  other arithmetic  103 us (40%)
  local copies, waits for them, and re-layouts  72.9 us (29%)
  waiting for transfers between devices  38.9 us (15%)
  blocking collectives  22.9 us (9%)
  between operations  13.7 us (5%)
  starting transfers between devices  3.8 us (1%)
    gather x8, local copies, waits for them, and re-layouts, corner(): return jnp.take(flattened, flat_index + shift_by, axis=1)  63.9 us
    scatter-add x1, other arithmetic, spread(): result = result.at[:, flat_index + width + 1].add(frac_col * lower_part)  23.4 us
    scatter-add x1, other arithmetic, spread(): result = result.at[:, flat_index + 1].add(frac_col * upper_part)  23.3 us
    scatter-add x1, other arithmetic, spread(): result = result.at[:, flat_index + width].add((1.0 - frac_col) * lower_part)  23.3 us
    scatter-add x1, other arithmetic, spread(): result = result.at[:, flat_index].add((1.0 - frac_col) * upper_part)  23 us
    all_gather x1, blocking collectives, per_device(): full_cotangent = lax.all_gather(cotangent, 'view', axis=1, tiled=True)  22.9 us
    psum x1, waiting for transfers between devices, per_device(): view_sum = lax.psum(warped, 'view')  22.7 us
    reduce_scatter x1, waiting for transfers between devices, depth_reduce(): lax.psum_scatter(partial_grad, 'depth', scatter_dimension=2, tiled=True)  14.6 us
  transfers between devices with their start and end apart: 5, of which 4 were waited for; matrix products, arithmetic and copies ran while one was open for 1% of the time, Pallas kernels for 0%

commit v1 on v0

v1 whole, which is shorter than its diff:
```python
import functools

import jax
import jax.numpy as jnp
from jax import lax
from jax.experimental import pallas as pl
from jax.experimental.pallas import tpu as pltpu
from jax.sharding import PartitionSpec as P

MESH = pl.DeviceIdType.MESH
F32 = jnp.float32
BF16 = jnp.bfloat16
TILE = 256
CHUNK = 64
KEEP_BYTES = 24 << 20


def split(value):
    high = value.astype(BF16)
    low = (value - high.astype(F32)).astype(BF16)
    return jnp.concatenate([high, low], axis=0)


def kernel(
    sizes, feat, cot, srow, scol, frac, out,
    fbuf, rbuf, cbuf, wbuf, cotv, lane_q, stack, fstack, mats, warp, rweight, total, outbuf, inbuf,
    local_sem, f_send, f_recv, i_send, i_recv, o_send, o_recv, o_local,
):
    views, depths, rows, cc, planes, rl, width, keep = sizes
    me = lax.axis_index("view")
    mx = lax.axis_index("depth")
    mr = lax.axis_index("row")
    height = rows * rl
    wx = width // depths
    factor = 2.0 / views

    def view_at(step):
        return lax.rem(me + step, views)

    def others(step):
        for dx in range(depths):
            for dr in range(rows):
                yield dx, dr, lax.rem(mx + dx, depths), lax.rem(mr + dr, rows)

    barrier = pltpu.get_barrier_semaphore()
    for dx, dr, x, r in others(0):
        if dx or dr:
            pl.semaphore_signal(barrier, inc=1, device_id={"view": me, "depth": x, "row": r}, device_id_type=MESH)

    @pl.loop(1, views)
    def _(step):
        for dx, dr, x, r in others(step):
            pl.semaphore_signal(
                barrier, inc=1, device_id={"view": view_at(step), "depth": x, "row": r}, device_id_type=MESH
            )

    local = [
        pltpu.make_async_copy(feat.at[0, pl.ds(me * cc, cc)], fbuf.at[me, mr], local_sem.at[0]),
        pltpu.make_async_copy(srow.at[0], rbuf.at[me], local_sem.at[1]),
        pltpu.make_async_copy(scol.at[0], cbuf.at[me], local_sem.at[2]),
        pltpu.make_async_copy(frac.at[:, 0], wbuf.at[me], local_sem.at[3]),
        pltpu.make_async_copy(cot, cotv, local_sem.at[4]),
    ]
    for copy in local:
        copy.start()
    for j in range(TILE // CHUNK):
        part = lax.broadcasted_iota(jnp.int32, (CHUNK, width), 0) + j * CHUNK
        lane_q[pl.ds(j * CHUNK, CHUNK), :] = part.astype(F32).astype(BF16)

    pl.semaphore_wait(barrier, views * depths * rows - 1)

    def feat_copy(step, dr):
        to, r = lax.rem(me + views - step, views), lax.rem(mr + dr, rows)
        return pltpu.make_async_remote_copy(
            src_ref=feat.at[0, pl.ds(to * cc, cc)], dst_ref=fbuf.at[me, mr],
            send_sem=f_send.at[step, dr], recv_sem=f_recv.at[step, dr],
            device_id={"view": to, "row": r}, device_id_type=MESH,
        )

    def index_copies(step):
        to = lax.rem(me + views - step, views)
        pairs = [(srow.at[0], rbuf.at[me]), (scol.at[0], cbuf.at[me]), (frac.at[:, 0], wbuf.at[me])]
        return [
            pltpu.make_async_remote_copy(
                src_ref=source, dst_ref=target,
                send_sem=i_send.at[step, at], recv_sem=i_recv.at[step, at],
                device_id={"view": to}, device_id_type=MESH,
            )
            for at, (source, target) in enumerate(pairs)
        ]

    for dr in range(1, rows):
        feat_copy(0, dr).start()

    @pl.loop(1, views)
    def _(step):
        for dr in range(rows):
            feat_copy(step, dr).start()
        for copy in index_copies(step):
            copy.start()

    row_of = (lax.broadcasted_iota(jnp.int32, (height * cc, width), 0) // cc).astype(F32)

    def build(slot, v, d, i):
        col = cbuf[v, d, pl.ds(i, 1), :].astype(F32)
        fx = (wbuf[v, 1, d, pl.ds(i, 1), :].astype(F32) / 256.0).astype(BF16)
        fx = jnp.broadcast_to(fx, (CHUNK, width))
        for t in range(width // TILE):
            c = jnp.broadcast_to((col - float(t * TILE)).astype(BF16), (CHUNK, width))
            for j in range(TILE // CHUNK):
                apart = (lane_q[pl.ds(j * CHUNK, CHUNK), :] - c) - fx
                mats[slot, pl.ds(t * TILE + j * CHUNK, CHUNK), :] = jnp.maximum(
                    BF16(1.0) - jnp.abs(apart), BF16(0.0)
                )

    def slot_of(v, d, i):
        return (v * planes + d) * rl + i if keep else i

    def forward(v):
        for s in range(rows):
            for i in range(rl):
                stack[pl.ds((s * rl + i) * cc, cc), :] = fbuf[v, s, :, i, :]
        fstack[...] = split(stack[...])

        @pl.loop(0, planes)
        def _(d):
            for i in range(rl):
                slot = slot_of(v, d, i)
                build(slot, v, d, i)
                row = rbuf[v, d, pl.ds(i, 1), :].astype(F32)
                fy = wbuf[v, 0, d, pl.ds(i, 1), :].astype(F32) / 256.0
                weight = jnp.maximum(1.0 - jnp.abs(row_of - (row + fy)), 0.0)
                both = jnp.dot(fstack[...], mats[slot], preferred_element_type=F32)
                mixed = (both[: height * cc] + both[height * cc :]) * weight
                warped = mixed[:cc]
                for h in range(1, height):
                    warped = warped + mixed[h * cc : (h + 1) * cc]
                warp[v, d, i] = warped

    for copy in local[:4]:
        copy.wait()
    for dr in range(1, rows):
        feat_copy(0, dr).wait_recv()
    forward(me)

    @pl.loop(1, views)
    def _(step):
        for dr in range(rows):
            feat_copy(step, dr).wait_recv()
        for copy in index_copies(step):
            copy.wait_recv()
        forward(view_at(step))

    local[4].wait()

    def out_copy(v, step, dx, dr):
        x, r = lax.rem(mx + dx, depths), lax.rem(mr + dr, rows)
        return pltpu.make_async_remote_copy(
            src_ref=outbuf.at[v, x, r], dst_ref=inbuf.at[me, mx, mr],
            send_sem=o_send.at[step, dx, dr], recv_sem=o_recv.at[step, dx, dr],
            device_id={"view": v, "depth": x, "row": r}, device_id_type=MESH,
        )

    @pl.loop(0, planes)
    def _(d):
        for i in range(rl):
            mean = lax.fori_loop(1, views, lambda v, run: run + warp[v, d, i], warp[0, d, i]) / views
            grad = factor * cotv[d, :, i, :]

            def each(v, _):
                warp[v, d, i] = grad * (warp[v, d, i] - mean)
                return 0

            lax.fori_loop(0, views, each, 0)

    def backward(v):
        total[...] = jnp.zeros_like(total)

        @pl.loop(0, planes)
        def _(d):
            for i in range(rl):
                slot = slot_of(v, d, i)
                if not keep:
                    build(slot, v, d, i)
                row = rbuf[v, d, pl.ds(i, 1), :].astype(F32)
                fy = wbuf[v, 0, d, pl.ds(i, 1), :].astype(F32) / 256.0
                weight = jnp.maximum(1.0 - jnp.abs(row_of - (row + fy)), 0.0)
                moved = jnp.concatenate([warp[v, d, i]] * height, axis=0) * weight
                both = lax.dot_general(
                    split(moved), mats[slot], (((1,), (1,)), ((), ())), preferred_element_type=F32
                )
                total[...] += both[: height * cc] + both[height * cc :]

        for x in range(depths):
            for s in range(rows):
                for i in range(rl):
                    outbuf[v, x, s, i] = total[pl.ds((s * rl + i) * cc, cc), pl.ds(x * wx, wx)]

    @pl.loop(1, views)
    def _(step):
        v = view_at(step)
        backward(v)
        for dx in range(depths):
            for dr in range(rows):
                out_copy(v, step, dx, dr).start()

    backward(me)
    for dx in range(depths):
        for dr in range(rows):
            if dx or dr:
                out_copy(me, 0, dx, dr).start()
    for dx in range(depths):
        for dr in range(rows):
            if dx or dr:
                out_copy(me, 0, dx, dr).wait_recv()

    @pl.loop(1, views)
    def _(step):
        for dx in range(depths):
            for dr in range(rows):
                out_copy(view_at(step), step, dx, dr).wait_recv()

    for i in range(rl):
        for u in range(views):
            piece = None
            for x in range(depths):
                for s in range(rows):
                    own = jnp.logical_and(jnp.logical_and(me == u, mx == x), mr == s)
                    term = jnp.where(own, outbuf[u, x, s, i], inbuf[u, x, s, i])
                    piece = term if piece is None else piece + term
            out[i, pl.ds(u * cc, cc), :] = piece

    for dr in range(1, rows):
        feat_copy(0, dr).wait_send()
    for dx in range(depths):
        for dr in range(rows):
            if dx or dr:
                out_copy(me, 0, dx, dr).wait_send()

    @pl.loop(1, views)
    def _(step):
        for dr in range(rows):
            feat_copy(step, dr).wait_send()
        for copy in index_copies(step):
            copy.wait_send()
        for dx in range(depths):
            for dr in range(rows):
                out_copy(view_at(step), step, dx, dr).wait_send()


def per_device(features, cotangent, src_row, src_col, fractions):
    views, depths, rows = (lax.axis_size(axis) for axis in ("view", "depth", "row"))
    channels, rl, width = features.shape[1:]
    planes, cc = cotangent.shape[:2]
    height, wx = rows * rl, width // depths
    matrices = views * planes * rl
    keep = matrices * width * width * 2 <= KEEP_BYTES
    sizes = (views, depths, rows, cc, planes, rl, width, keep)
    grad = pl.pallas_call(
        functools.partial(kernel, sizes),
        out_shape=jax.ShapeDtypeStruct((rl, channels, wx), F32),
        in_specs=[pl.BlockSpec(memory_space=pl.ANY)] * 5,
        out_specs=pl.BlockSpec(memory_space=pltpu.VMEM),
        scratch_shapes=[
            pltpu.VMEM((views, rows, cc, rl, width), F32),
            pltpu.VMEM((views, planes, rl, width), jnp.int32),
            pltpu.VMEM((views, planes, rl, width), jnp.int32),
            pltpu.VMEM((views, 2, planes, rl, width), jnp.int32),
            pltpu.VMEM((planes, cc, rl, width), F32),
            pltpu.VMEM((TILE, width), BF16),
            pltpu.VMEM((height * cc, width), F32),
            pltpu.VMEM((2 * height * cc, width), BF16),
            pltpu.VMEM((matrices if keep else rl, width, width), BF16),
            pltpu.VMEM((views, planes, rl, cc, width), F32),
            pltpu.VMEM((8, width), F32),
            pltpu.VMEM((height * cc, width), F32),
            pltpu.VMEM((views, depths, rows, rl, cc, wx), F32),
            pltpu.VMEM((views, depths, rows, rl, cc, wx), F32),
            pltpu.SemaphoreType.DMA((5,)),
            pltpu.SemaphoreType.DMA((views, rows)),
            pltpu.SemaphoreType.DMA((views, rows)),
            pltpu.SemaphoreType.DMA((views, 3)),
            pltpu.SemaphoreType.DMA((views, 3)),
            pltpu.SemaphoreType.DMA((views, depths, rows)),
            pltpu.SemaphoreType.DMA((views, depths, rows)),
            pltpu.SemaphoreType.DMA((1,)),
        ],
        compiler_params=pltpu.CompilerParams(
            collective_id=0, has_side_effects=True, vmem_limit_bytes=56 << 20
        ),
    )(features, cotangent, src_row, src_col, fractions)
    return jnp.transpose(grad, (1, 0, 2))[None]


def solution(mesh):
    in_specs = (
        P("view", None, ("group", "row"), None),
        P("depth", "view", ("group", "row"), None),
        P("view", "depth", ("group", "row"), None),
        P("view", "depth", ("group", "row"), None),
        P(None, "view", "depth", ("group", "row"), None),
    )
    out_specs = P("view", None, ("group", "row"), "depth")
    return jax.shard_map(
        per_device, mesh=mesh, in_specs=in_specs, out_specs=out_specs, check_vma=False
    )
```

time: 255 us -> 35.3 us (0.14)
  other arithmetic: 103 us -> 0 us
  local copies, waits for them, and re-layouts: 72.9 us -> 1.52 us
  waiting for transfers between devices: 38.9 us -> 0 us
  Pallas kernels: 0 us -> 33.6 us
  blocking collectives: 22.9 us -> 0 us
  between operations: 13.7 us -> 0.01 us
  starting transfers between devices: 3.8 us -> 0 us
    scatter-add x4 -> x0, other arithmetic: 93 us -> none  [the longest x1 23.4 us: spread(): result = result.at[:, flat_index + width + 1].add(frac_col * lower_part)]
    gather x8 -> x0, local copies, waits for them, and re-layouts: 63.9 us -> none  [corner(): return jnp.take(flattened, flat_index + shift_by, axis=1)]
    pallas_call x0 -> x1, Pallas kernels: none -> 33.6 us  [per_device(): pl.pallas_call(functools.partial(kernel, sizes), out_shape=jax.ShapeDtype...]
    all_gather x1 -> x0, blocking collectives: 22.9 us -> none  [per_device(): full_cotangent = lax.all_gather(cotangent, 'view', axis=1, tiled=True)]
    psum x1 -> x0, waiting for transfers between devices: 22.7 us -> none  [per_device(): view_sum = lax.psum(warped, 'view')]
    reduce_scatter x1 -> x0, waiting for transfers between devices: 14.6 us -> none  [depth_reduce(): lax.psum_scatter(partial_grad, 'depth', scatter_dimension=2, tiled=True)]
    mul x4 -> x0, local copies, waits for them, and re-layouts: 6.99 us -> none  [the longest x1 1.78 us: spread(): result = result.at[:, flat_index].add((1.0 - frac_col) * upper_part)]
    ppermute x3 -> x0, starting transfers between devices: 3.76 us -> none  [the longest x1 2.39 us: with_halo(): lax.ppermute(lax.slice_in_dim(block, block.shape[dim] - width, None, axis...]
  transfers between devices with their start and end apart: 5 -> 0, of which waited for: 4 -> 0; matrix products, arithmetic and copies ran while one was open for 1% -> 0% of each run, Pallas kernels for 0% -> 0%
where the time goes in v1:
time: 35.3 us; the launch traced here: 35.2 us
  Pallas kernels  33.6 us (95%)
  local copies, waits for them, and re-layouts  1.52 us (4%)
    pallas_call x1, Pallas kernels, per_device(): pl.pallas_call(functools.partial(kernel, sizes), out_shape=jax.ShapeDtype...  33.6 us
    broadcast_in_dim x1, local copies, waits for them, and re-layouts, per_device(): return jnp.transpose(grad, (1, 0, 2))[None]  1.52 us

profile of v1, /device:TPU:0, one launch (start us, length us, event | category | flops | bytes accessed | tf_op | source)
XLA Modules:
  0.0 35.2 jit_solution(1434222326788332552)
XLA Ops:
  0.0 33.6 %shard_map.55 = f32[2,32,256]{2,1,0:T(8,128)} custom-call(f32[1,32,2,512]{3,2,1,0:T(2,128)} %feat.1, f32[4,8,2,512]{3,2,1,0:T(2,128)} %cot.1, s32[1,4,2,512]{3,2,1,0:T(2,128)} %srow.1, s32[1,4,2,512]{3,2,1,0:T(2,128)} %scol.1, s32[2,1,4,2,512]{4,3,2,1,0:T(2,128)} %frac.1), custom_call_target="tpu_custom_call" | custom-call | tf_op jit(solution)/shard_map/pallas_call | solution.py:259
  33.6 1.5 %copy.6 = f32[1,32,2,256]{3,2,1,0:T(2,128)} copy(f32[1,32,2,256]{3,1,2,0:T(8,128)} %bitcast.3) | data formatting | bytes 131072 | tf_op jit(solution)/shard_map/broadcast_in_dim | solution.py:292

commit v2 on v1

v2 whole, which is shorter than its diff:
```python
import functools

import jax
import jax.numpy as jnp
from jax import lax
from jax.experimental import pallas as pl
from jax.experimental.pallas import tpu as pltpu
from jax.sharding import PartitionSpec as P

MESH = pl.DeviceIdType.MESH
F32 = jnp.float32
BF16 = jnp.bfloat16
TILE = 256
CHUNK = 64
KEEP_BYTES = 24 << 20


def split(value):
    high = value.astype(BF16)
    low = (value - high.astype(F32)).astype(BF16)
    return jnp.concatenate([high, low], axis=0)


def kernel(
    sizes, feat, cot, srow, scol, frac, out,
    fown, fbuf, rbuf, cbuf, wbuf, cotv, lane_q, stack, mats, warp, wsum, cotg, outbuf, pbuf, red, inbuf,
    local_sem, f_send, f_recv, p_send, p_recv, i_send, i_recv, d_send, d_recv, o_send, o_recv,
):
    views, depths, rows, cc, planes, rl, width, keep = sizes
    me = lax.axis_index("view")
    mx = lax.axis_index("depth")
    mr = lax.axis_index("row")
    height = rows * rl
    wx = width // depths
    factor = 2.0 / views

    def view_at(step):
        return lax.rem(me + step, views)

    def row_at(step):
        return lax.rem(mr + step, rows)

    def depth_at(step):
        return lax.rem(mx + step, depths)

    barrier = pltpu.get_barrier_semaphore()

    def greet(v, x, r):
        pl.semaphore_signal(
            barrier, inc=1, device_id={"view": v, "depth": x, "row": r}, device_id_type=MESH
        )

    @pl.loop(1, views)
    def _(step):
        for dx in range(depths):
            greet(view_at(step), depth_at(dx), mr)

    for dx in range(1, depths):
        greet(me, depth_at(dx), mr)
    for dr in range(1, rows):
        greet(me, mx, row_at(dr))

    local = [
        pltpu.make_async_copy(feat.at[0], fown, local_sem.at[0]),
        pltpu.make_async_copy(feat.at[0, pl.ds(me * cc, cc)], fbuf.at[me, mr], local_sem.at[1]),
        pltpu.make_async_copy(srow.at[0], rbuf.at[me], local_sem.at[2]),
        pltpu.make_async_copy(scol.at[0], cbuf.at[me], local_sem.at[3]),
        pltpu.make_async_copy(frac.at[:, 0], wbuf.at[me], local_sem.at[4]),
        pltpu.make_async_copy(cot, cotv, local_sem.at[5]),
    ]
    for copy in local:
        copy.start()
    for j in range(TILE // CHUNK):
        part = lax.broadcasted_iota(jnp.int32, (CHUNK, width), 0) + j * CHUNK
        lane_q[pl.ds(j * CHUNK, CHUNK), :] = part.astype(F32).astype(BF16)
    row_of = (lax.broadcasted_iota(jnp.int32, (height * cc, width), 0) // cc).astype(F32)

    def feat_copy(step):
        to = lax.rem(me + views - step, views)
        return pltpu.make_async_remote_copy(
            src_ref=fown.at[pl.ds(to * cc, cc)], dst_ref=fbuf.at[me, mr],
            send_sem=f_send.at[step], recv_sem=f_recv.at[step],
            device_id={"view": to}, device_id_type=MESH,
        )

    def pass_copy(step, dr):
        block = fbuf.at[view_at(step), mr]
        return pltpu.make_async_remote_copy(
            src_ref=block, dst_ref=block,
            send_sem=p_send.at[step, dr], recv_sem=p_recv.at[step, dr],
            device_id={"row": row_at(dr)}, device_id_type=MESH,
        )

    def index_copies(step):
        to = lax.rem(me + views - step, views)
        return [
            pltpu.make_async_remote_copy(
                src_ref=block.at[me], dst_ref=block.at[me],
                send_sem=i_send.at[step, at], recv_sem=i_recv.at[step, at],
                device_id={"view": to}, device_id_type=MESH,
            )
            for at, block in enumerate((rbuf, cbuf, wbuf))
        ]

    def build(slot, v, d, i):
        col = cbuf[v, d, pl.ds(i, 1), :].astype(F32)
        fx = (wbuf[v, 1, d, pl.ds(i, 1), :].astype(F32) / 256.0).astype(BF16)
        fx = jnp.broadcast_to(fx, (CHUNK, width))
        for t in range(width // TILE):
            c = jnp.broadcast_to((col - float(t * TILE)).astype(BF16), (CHUNK, width))
            for j in range(TILE // CHUNK):
                apart = (lane_q[pl.ds(j * CHUNK, CHUNK), :] - c) - fx
                mats[slot, pl.ds(t * TILE + j * CHUNK, CHUNK), :] = jnp.maximum(
                    BF16(1.0) - jnp.abs(apart), BF16(0.0)
                )

    def slot_of(v, d, i):
        at = d * rl + i
        return v * (planes * rl) + at if keep else at

    def row_weight(v, d, i):
        row = rbuf[v, d, pl.ds(i, 1), :].astype(F32)
        fy = wbuf[v, 0, d, pl.ds(i, 1), :].astype(F32) / 256.0
        return jnp.maximum(1.0 - jnp.abs(row_of - (row + fy)), 0.0)

    def build_all(v):
        for d in range(planes):
            for i in range(rl):
                build(slot_of(v, d, i), v, d, i)

    def sampled(v, first):
        for s in range(rows):
            for i in range(rl):
                stack[pl.ds((s * rl + i) * cc, cc), :] = fbuf[v, s, :, i, :]
        both_parts = split(stack[...])
        for d in range(planes):
            for i in range(rl):
                if not first:
                    build(slot_of(v, d, i), v, d, i)
                both = jnp.dot(both_parts, mats[slot_of(v, d, i)], preferred_element_type=F32)
                mixed = (both[: height * cc] + both[height * cc :]) * row_weight(v, d, i)
                warped = mixed[:cc]
                for h in range(1, height):
                    warped = warped + mixed[h * cc : (h + 1) * cc]
                warp[v, d, i] = warped
                wsum[d, i] = warped if first else wsum[d, i] + warped

    for copy in local[2:5]:
        copy.wait()
    build_all(me)
    for copy in local[:2]:
        copy.wait()
    pl.semaphore_wait(barrier, views * depths + rows - 2)

    for dr in range(1, rows):
        pass_copy(0, dr).start()

    @pl.loop(1, views)
    def _(step):
        feat_copy(step).start()

    @pl.loop(1, views)
    def _(step):
        for copy in index_copies(step):
            copy.start()

    local[5].wait()
    for d in range(planes):
        for i in range(rl):
            cotg[d, i] = factor * cotv[d, :, i, :]
    for dr in range(1, rows):
        pass_copy(0, dr).wait_recv()
    sampled(me, True)

    @pl.loop(1, views)
    def _(step):
        feat_copy(step).wait_recv()
        for dr in range(1, rows):
            pass_copy(step, dr).start()

    @pl.loop(1, views)
    def _(step):
        for copy in index_copies(step):
            copy.wait_recv()
        for dr in range(1, rows):
            pass_copy(step, dr).wait_recv()
        sampled(view_at(step), False)

    def backward(v):
        if not keep:
            build_all(v)
        both = None
        for d in range(planes):
            for i in range(rl):
                grad = cotg[d, i] * (warp[v, d, i] - wsum[d, i] / views)
                moved = jnp.concatenate([grad] * height, axis=0) * row_weight(v, d, i)
                term = lax.dot_general(
                    split(moved), mats[slot_of(v, d, i)], (((1,), (1,)), ((), ())),
                    preferred_element_type=F32,
                )
                both = term if both is None else both + term
        total = both[: height * cc] + both[height * cc :]
        for s in range(rows):
            for x in range(depths):
                for i in range(rl):
                    at = (s * rl + i) * cc
                    outbuf[v, s, x, i] = total[at : at + cc, x * wx : (x + 1) * wx]

    def core_copy(v, dr):
        r = row_at(dr)
        return pltpu.make_async_remote_copy(
            src_ref=outbuf.at[v, r], dst_ref=pbuf.at[v, dr],
            send_sem=d_send.at[v, dr], recv_sem=d_recv.at[v, dr],
            device_id={"row": r}, device_id_type=MESH,
        )

    def out_copy(v, step, dx):
        x = depth_at(dx)
        return pltpu.make_async_remote_copy(
            src_ref=red.at[v, x], dst_ref=inbuf.at[me, mx],
            send_sem=o_send.at[step, dx], recv_sem=o_recv.at[step, dx],
            device_id={"view": v, "depth": x}, device_id_type=MESH,
        )

    def start_core(v):
        for dr in range(1, rows):
            core_copy(v, dr).start()

    def add_cores(v, target, x):
        piece = outbuf[v, mr, x]
        for dr in range(1, rows):
            piece = piece + pbuf[v, dr, x]
        target[...] = piece

    def pass_on(step):
        v = view_at(step)
        for dr in range(1, rows):
            core_copy(v, dr).wait_recv()
        for x in range(depths):
            add_cores(v, red.at[v, x], x)
        for dx in range(depths):
            out_copy(v, step, dx).start()

    @pl.loop(1, views)
    def _(step):
        v = view_at(step)
        backward(v)
        start_core(v)

        @pl.when(step > 1)
        def _():
            pass_on(step - 1)

    backward(me)
    start_core(me)
    if views > 1:
        pass_on(views - 1)
    for dr in range(1, rows):
        core_copy(me, dr).wait_recv()
    for dx in range(1, depths):
        add_cores(me, red.at[me, depth_at(dx)], depth_at(dx))
        out_copy(me, 0, dx).start()
    add_cores(me, inbuf.at[me, mx], mx)

    @pl.loop(1, views)
    def _(step):
        for dx in range(depths):
            out_copy(view_at(step), step, dx).wait_recv()

    for dx in range(1, depths):
        out_copy(me, 0, dx).wait_recv()

    for i in range(rl):
        for u in range(views):
            piece = inbuf[u, 0, i]
            for x in range(1, depths):
                piece = piece + inbuf[u, x, i]
            out[i, pl.ds(u * cc, cc), :] = piece

    for dr in range(1, rows):
        pass_copy(0, dr).wait_send()
        core_copy(me, dr).wait_send()
    for dx in range(1, depths):
        out_copy(me, 0, dx).wait_send()

    @pl.loop(1, views)
    def _(step):
        feat_copy(step).wait_send()
        for copy in index_copies(step):
            copy.wait_send()
        for dr in range(1, rows):
            pass_copy(step, dr).wait_send()
            core_copy(view_at(step), dr).wait_send()
        for dx in range(depths):
            out_copy(view_at(step), step, dx).wait_send()


def per_device(features, cotangent, src_row, src_col, fractions):
    views, depths, rows = (lax.axis_size(axis) for axis in ("view", "depth", "row"))
    channels, rl, width = features.shape[1:]
    planes, cc = cotangent.shape[:2]
    height, wx = rows * rl, width // depths
    matrices = views * planes * rl
    keep = matrices * width * width * 2 <= KEEP_BYTES
    sizes = (views, depths, rows, cc, planes, rl, width, keep)
    grad = pl.pallas_call(
        functools.partial(kernel, sizes),
        out_shape=jax.ShapeDtypeStruct((rl, channels, wx), F32),
        in_specs=[pl.BlockSpec(memory_space=pl.ANY)] * 5,
        out_specs=pl.BlockSpec(memory_space=pltpu.VMEM),
        scratch_shapes=[
            pltpu.VMEM((channels, rl, width), F32),
            pltpu.VMEM((views, rows, cc, rl, width), F32),
            pltpu.VMEM((views, planes, rl, width), jnp.int32),
            pltpu.VMEM((views, planes, rl, width), jnp.int32),
            pltpu.VMEM((views, 2, planes, rl, width), jnp.int32),
            pltpu.VMEM((planes, cc, rl, width), F32),
            pltpu.VMEM((TILE, width), BF16),
            pltpu.VMEM((height * cc, width), F32),
            pltpu.VMEM((matrices if keep else planes * rl, width, width), BF16),
            pltpu.VMEM((views, planes, rl, cc, width), F32),
            pltpu.VMEM((planes, rl, cc, width), F32),
            pltpu.VMEM((planes, rl, cc, width), F32),
            pltpu.VMEM((views, rows, depths, rl, cc, wx), F32),
            pltpu.VMEM((views, rows, depths, rl, cc, wx), F32),
            pltpu.VMEM((views, depths, rl, cc, wx), F32),
            pltpu.VMEM((views, depths, rl, cc, wx), F32),
            pltpu.SemaphoreType.DMA((6,)),
            pltpu.SemaphoreType.DMA((views,)),
            pltpu.SemaphoreType.DMA((views,)),
            pltpu.SemaphoreType.DMA((views, rows)),
            pltpu.SemaphoreType.DMA((views, rows)),
            pltpu.SemaphoreType.DMA((views, 3)),
            pltpu.SemaphoreType.DMA((views, 3)),
            pltpu.SemaphoreType.DMA((views, rows)),
            pltpu.SemaphoreType.DMA((views, rows)),
            pltpu.SemaphoreType.DMA((views, depths)),
            pltpu.SemaphoreType.DMA((views, depths)),
        ],
        compiler_params=pltpu.CompilerParams(
            collective_id=0, has_side_effects=True, vmem_limit_bytes=56 << 20
        ),
    )(features, cotangent, src_row, src_col, fractions)
    return jnp.transpose(grad, (1, 0, 2))[None]


def solution(mesh):
    in_specs = (
        P("view", None, ("group", "row"), None),
        P("depth", "view", ("group", "row"), None),
        P("view", "depth", ("group", "row"), None),
        P("view", "depth", ("group", "row"), None),
        P(None, "view", "depth", ("group", "row"), None),
    )
    out_specs = P("view", None, ("group", "row"), "depth")
    return jax.shard_map(
        per_device, mesh=mesh, in_specs=in_specs, out_specs=out_specs, check_vma=False
    )
```

time: 35.3 us -> 30.2 us (0.86)
  Pallas kernels: 33.6 us -> 28.5 us
    pallas_call x1, Pallas kernels: 33.6 us -> 28.5 us  [per_device(): pl.pallas_call(functools.partial(kernel, sizes), out_shape=jax.ShapeDtype...]
where the time goes in v2:
time: 30.2 us; the launch traced here: 30.1 us
  Pallas kernels  28.5 us (94%)
  local copies, waits for them, and re-layouts  1.52 us (5%)
    pallas_call x1, Pallas kernels, per_device(): pl.pallas_call(functools.partial(kernel, sizes), out_shape=jax.ShapeDtype...  28.5 us
    broadcast_in_dim x1, local copies, waits for them, and re-layouts, per_device(): return jnp.transpose(grad, (1, 0, 2))[None]  1.52 us

profile of v2, /device:TPU:0, one launch (start us, length us, event | category | flops | bytes accessed | tf_op | source)
XLA Modules:
  0.0 30.1 jit_solution(2255722086935811623)
XLA Ops:
  0.0 28.5 %shard_map.55 = f32[2,32,256]{2,1,0:T(8,128)} custom-call(f32[1,32,2,512]{3,2,1,0:T(2,128)} %feat.1, f32[4,8,2,512]{3,2,1,0:T(2,128)} %cot.1, s32[1,4,2,512]{3,2,1,0:T(2,128)} %srow.1, s32[1,4,2,512]{3,2,1,0:T(2,128)} %scol.1, s32[2,1,4,2,512]{4,3,2,1,0:T(2,128)} %frac.1), custom_call_target="tpu_custom_call" | custom-call | tf_op jit(solution)/shard_map/pallas_call | solution.py:306
  28.5 1.5 %copy.6 = f32[1,32,2,256]{3,2,1,0:T(2,128)} copy(f32[1,32,2,256]{3,1,2,0:T(8,128)} %bitcast.3) | data formatting | bytes 131072 | tf_op jit(solution)/shard_map/broadcast_in_dim | solution.py:344

commit v3 on v2

--- a/solution.py
+++ b/solution.py
@@ -23,10 +23,10 @@
 
 def kernel(
     sizes, feat, cot, srow, scol, frac, out,
-    fown, fbuf, rbuf, cbuf, wbuf, cotv, lane_q, stack, mats, warp, wsum, cotg, outbuf, pbuf, red, inbuf,
+    fown, fbuf, rbuf, cbuf, wbuf, cotv, lane_q, stack, mats, warp, wsum, cotg, fstack, partial, outbuf, pbuf, red, inbuf,
     local_sem, f_send, f_recv, p_send, p_recv, i_send, i_recv, d_send, d_recv, o_send, o_recv,
 ):
-    views, depths, rows, cc, planes, rl, width, keep = sizes
+    views, depths, rows, cc, planes, rl, width, keep, groups = sizes
     me = lax.axis_index("view")
     mx = lax.axis_index("depth")
     mr = lax.axis_index("row")
@@ -91,15 +91,19 @@
             device_id={"row": row_at(dr)}, device_id_type=MESH,
         )
 
-    def index_copies(step):
+    per_group = planes // groups
+
+    def index_copies(step, group):
         to = lax.rem(me + views - step, views)
+        part = pl.ds(group * per_group, per_group)
+        blocks = (rbuf.at[me, part], cbuf.at[me, part], wbuf.at[me, 0, part], wbuf.at[me, 1, part])
         return [
             pltpu.make_async_remote_copy(
-                src_ref=block.at[me], dst_ref=block.at[me],
-                send_sem=i_send.at[step, at], recv_sem=i_recv.at[step, at],
+                src_ref=block, dst_ref=block,
+                send_sem=i_send.at[step, group, at], recv_sem=i_recv.at[step, group, at],
                 device_id={"view": to}, device_id_type=MESH,
             )
-            for at, block in enumerate((rbuf, cbuf, wbuf))
+            for at, block in enumerate(blocks)
         ]
 
     def build(slot, v, d, i):
@@ -123,21 +127,26 @@
         fy = wbuf[v, 0, d, pl.ds(i, 1), :].astype(F32) / 256.0
         return jnp.maximum(1.0 - jnp.abs(row_of - (row + fy)), 0.0)
 
-    def build_all(v):
-        for d in range(planes):
+    def planes_of(group):
+        return range(group * per_group, (group + 1) * per_group)
+
+    def build_all(v, plane_list):
+        for d in plane_list:
             for i in range(rl):
                 build(slot_of(v, d, i), v, d, i)
 
-    def sampled(v, first):
+    def load_features(v):
         for s in range(rows):
             for i in range(rl):
                 stack[pl.ds((s * rl + i) * cc, cc), :] = fbuf[v, s, :, i, :]
-        both_parts = split(stack[...])
-        for d in range(planes):
+        fstack[v] = split(stack[...])
+
+    def sampled(v, plane_list, first):
+        for d in plane_list:
             for i in range(rl):
                 if not first:
                     build(slot_of(v, d, i), v, d, i)
-                both = jnp.dot(both_parts, mats[slot_of(v, d, i)], preferred_element_type=F32)
+                both = jnp.dot(fstack[v], mats[slot_of(v, d, i)], preferred_element_type=F32)
                 mixed = (both[: height * cc] + both[height * cc :]) * row_weight(v, d, i)
                 warped = mixed[:cc]
                 for h in range(1, height):
@@ -147,7 +156,7 @@
 
     for copy in local[2:5]:
         copy.wait()
-    build_all(me)
+    build_all(me, range(planes))
     for copy in local[:2]:
         copy.wait()
     pl.semaphore_wait(barrier, views * depths + rows - 2)
@@ -159,10 +168,12 @@
     def _(step):
         feat_copy(step).start()
 
-    @pl.loop(1, views)
-    def _(step):
-        for copy in index_copies(step):
-            copy.start()
+    for group in range(groups):
+
+        @pl.loop(1, views)
+        def _(step):
+            for copy in index_copies(step, group):
+                copy.start()
 
     local[5].wait()
     for d in range(planes):
@@ -170,7 +181,8 @@
             cotg[d, i] = factor * cotv[d, :, i, :]
     for dr in range(1, rows):
         pass_copy(0, dr).wait_recv()
-    sampled(me, True)
+    load_features(me)
+    sampled(me, range(planes), True)
 
     @pl.loop(1, views)
     def _(step):
@@ -178,19 +190,22 @@
         for dr in range(1, rows):
             pass_copy(step, dr).start()
 
-    @pl.loop(1, views)
-    def _(step):
-        for copy in index_copies(step):
-            copy.wait_recv()
-        for dr in range(1, rows):
-            pass_copy(step, dr).wait_recv()
-        sampled(view_at(step), False)
-
-    def backward(v):
+    def gather_group(group):
+        @pl.loop(1, views)
+        def _(step):
+            for copy in index_copies(step, group):
+                copy.wait_recv()
+            if group == 0:
+                for dr in range(1, rows):
+                    pass_copy(step, dr).wait_recv()
+                load_features(view_at(step))
+            sampled(view_at(step), planes_of(group), False)
+
+    def adjoint(v, plane_list):
         if not keep:
-            build_all(v)
+            build_all(v, plane_list)
         both = None
-        for d in range(planes):
+        for d in plane_list:
             for i in range(rl):
                 grad = cotg[d, i] * (warp[v, d, i] - wsum[d, i] / views)
                 moved = jnp.concatenate([grad] * height, axis=0) * row_weight(v, d, i)
@@ -199,7 +214,22 @@
                     preferred_element_type=F32,
                 )
                 both = term if both is None else both + term
-        total = both[: height * cc] + both[height * cc :]
+        return both[: height * cc] + both[height * cc :]
+
+    for group in range(groups - 1):
+        gather_group(group)
+
+        @pl.loop(0, views)
+        def _(v):
+            term = adjoint(v, planes_of(group))
+            partial[v] = term if group == 0 else partial[v] + term
+
+    gather_group(groups - 1)
+
+    def backward(v):
+        total = adjoint(v, planes_of(groups - 1))
+        if groups > 1:
+            total = total + partial[v]
         for s in range(rows):
             for x in range(depths):
                 for i in range(rl):
@@ -286,8 +316,9 @@
     @pl.loop(1, views)
     def _(step):
         feat_copy(step).wait_send()
-        for copy in index_copies(step):
-            copy.wait_send()
+        for group in range(groups):
+            for copy in index_copies(step, group):
+                copy.wait_send()
         for dr in range(1, rows):
             pass_copy(step, dr).wait_send()
             core_copy(view_at(step), dr).wait_send()
@@ -302,7 +333,8 @@
     height, wx = rows * rl, width // depths
     matrices = views * planes * rl
     keep = matrices * width * width * 2 <= KEEP_BYTES
-    sizes = (views, depths, rows, cc, planes, rl, width, keep)
+    groups = 2 if planes % 2 == 0 else 1
+    sizes = (views, depths, rows, cc, planes, rl, width, keep, groups)
     grad = pl.pallas_call(
         functools.partial(kernel, sizes),
         out_shape=jax.ShapeDtypeStruct((rl, channels, wx), F32),
@@ -321,6 +353,8 @@
             pltpu.VMEM((views, planes, rl, cc, width), F32),
             pltpu.VMEM((planes, rl, cc, width), F32),
             pltpu.VMEM((planes, rl, cc, width), F32),
+            pltpu.VMEM((views, 2 * height * cc, width), BF16),
+            pltpu.VMEM((views, height * cc, width), F32),
             pltpu.VMEM((views, rows, depths, rl, cc, wx), F32),
             pltpu.VMEM((views, rows, depths, rl, cc, wx), F32),
             pltpu.VMEM((views, depths, rl, cc, wx), F32),
@@ -330,8 +364,8 @@
             pltpu.SemaphoreType.DMA((views,)),
             pltpu.SemaphoreType.DMA((views, rows)),
             pltpu.SemaphoreType.DMA((views, rows)),
-            pltpu.SemaphoreType.DMA((views, 3)),
-            pltpu.SemaphoreType.DMA((views, 3)),
+            pltpu.SemaphoreType.DMA((views, groups, 4)),
+            pltpu.SemaphoreType.DMA((views, groups, 4)),
             pltpu.SemaphoreType.DMA((views, rows)),
             pltpu.SemaphoreType.DMA((views, rows)),
             pltpu.SemaphoreType.DMA((views, depths)),

time: 30.2 us -> 31.6 us (1.046)
  Pallas kernels: 28.5 us -> 29.9 us
    pallas_call x1, Pallas kernels: 28.5 us -> 29.9 us  [per_device(): pl.pallas_call(functools.partial(kernel, sizes), out_shape=jax.ShapeDtype...]
where the time goes in v3:
time: 31.6 us; the launch traced here: 31.5 us
  Pallas kernels  29.9 us (95%)
  local copies, waits for them, and re-layouts  1.52 us (5%)
    pallas_call x1, Pallas kernels, per_device(): pl.pallas_call(functools.partial(kernel, sizes), out_shape=jax.ShapeDtype...  29.9 us
    broadcast_in_dim x1, local copies, waits for them, and re-layouts, per_device(): return jnp.transpose(grad, (1, 0, 2))[None]  1.52 us

profile of v3, /device:TPU:0, one launch (start us, length us, event | category | flops | bytes accessed | tf_op | source)
XLA Modules:
  0.0 31.5 jit_solution(14816361620040575375)
XLA Ops:
  0.0 29.9 %shard_map.55 = f32[2,32,256]{2,1,0:T(8,128)} custom-call(f32[1,32,2,512]{3,2,1,0:T(2,128)} %feat.1, f32[4,8,2,512]{3,2,1,0:T(2,128)} %cot.1, s32[1,4,2,512]{3,2,1,0:T(2,128)} %srow.1, s32[1,4,2,512]{3,2,1,0:T(2,128)} %scol.1, s32[2,1,4,2,512]{4,3,2,1,0:T(2,128)} %frac.1), custom_call_target="tpu_custom_call" | custom-call | tf_op jit(solution)/shard_map/pallas_call | solution.py:338
  30.0 1.5 %copy.6 = f32[1,32,2,256]{3,2,1,0:T(2,128)} copy(f32[1,32,2,256]{3,1,2,0:T(8,128)} %bitcast.3) | data formatting | bytes 131072 | tf_op jit(solution)/shard_map/broadcast_in_dim | solution.py:378

commit v4 on v2

--- a/solution.py
+++ b/solution.py
@@ -52,8 +52,7 @@
 
     @pl.loop(1, views)
     def _(step):
-        for dx in range(depths):
-            greet(view_at(step), depth_at(dx), mr)
+        greet(view_at(step), mx, mr)
 
     for dx in range(1, depths):
         greet(me, depth_at(dx), mr)
@@ -150,7 +149,7 @@
     build_all(me)
     for copy in local[:2]:
         copy.wait()
-    pl.semaphore_wait(barrier, views * depths + rows - 2)
+    pl.semaphore_wait(barrier, views + depths + rows - 3)
 
     for dr in range(1, rows):
         pass_copy(0, dr).start()

time: 30.2 us -> 30.2 us (level)
  no operation moved by 1% of the time
where the time goes in v4:
time: 30.2 us; the launch traced here: 30.1 us
  Pallas kernels  28.5 us (94%)
  local copies, waits for them, and re-layouts  1.52 us (5%)
    pallas_call x1, Pallas kernels, per_device(): pl.pallas_call(functools.partial(kernel, sizes), out_shape=jax.ShapeDtype...  28.5 us
    broadcast_in_dim x1, local copies, waits for them, and re-layouts, per_device(): return jnp.transpose(grad, (1, 0, 2))[None]  1.52 us

profile of v4, /device:TPU:0, one launch (start us, length us, event | category | flops | bytes accessed | tf_op | source)
XLA Modules:
  0.0 30.1 jit_solution(5285182163969386950)
XLA Ops:
  0.0 28.5 %shard_map.55 = f32[2,32,256]{2,1,0:T(8,128)} custom-call(f32[1,32,2,512]{3,2,1,0:T(2,128)} %feat.1, f32[4,8,2,512]{3,2,1,0:T(2,128)} %cot.1, s32[1,4,2,512]{3,2,1,0:T(2,128)} %srow.1, s32[1,4,2,512]{3,2,1,0:T(2,128)} %scol.1, s32[2,1,4,2,512]{4,3,2,1,0:T(2,128)} %frac.1), custom_call_target="tpu_custom_call" | custom-call | tf_op jit(solution)/shard_map/pallas_call | solution.py:305
  28.5 1.5 %copy.6 = f32[1,32,2,256]{3,2,1,0:T(2,128)} copy(f32[1,32,2,256]{3,1,2,0:T(8,128)} %bitcast.3) | data formatting | bytes 131072 | tf_op jit(solution)/shard_map/broadcast_in_dim | solution.py:343
